TPU v7x, 32 devices: a whole 2x2x4 slice. The times are simulated.
32 devices in a mesh: gx: 4 (over z), gy: 8 (over y, x, core).
Axes of the slice: x: 2, y: 2, z: 4, core: 2. Of those that a mesh axis runs over, the one named last changes fastest.
Arguments:
- tables: float32 [2, 262144, 128], P(None, ('gx', 'gy')), may hold values from -0.9 to 0.9
- cold_rows: int32 [32, 2, 32, 16], P(('gx', 'gy')), may hold values from 0 to 8191, as said below
- cold_bags: int32 [32, 2, 32, 16], P(('gx', 'gy')), may hold values from -1 to 127, as said below
- hot_rows: int32 [2, 256], replicated, may hold values from 0 to 262143
- hot_ids: int32 [4096, 2, 8], P(('gx', 'gy')), may hold values from 0 to 255
Outputs:
- pooled: float32 [4096, 2, 128], P(('gx', 'gy'))
Inputs may be any that keep to these rules, and one draw needn't show every extreme that they name: `cold_rows`: every entry names one of the owner's 8192 rows. `cold_bags`: live slots of one sender, table and owner come first, the empty ones (-1) after them; in every draw each table has an owner whose 16 slots are all live from every sender.
All inputs are finite; a program needn't handle non-finite values.
Results may differ from a plain program's by a relative error of at most 0.0003.
Values sent between devices are 32-bit elements; how exact they have to be, the bound alone decides.
No kernel may reach another device: no remote copies, remote signals or barrier semaphores. Data moves between devices by JAX's collectives and lax.ppermute only.
A program may use at most 64 MiB of HBM per device.

v0:
```python
import math
import jax
import jax.numpy as jnp
from jax import lax
from jax.sharding import PartitionSpec as P


def pick_rows(table, indices):
    count = indices.shape[0]
    block = math.gcd(512, count)
    row_ids = jnp.arange(table.shape[0], dtype=jnp.int32)
    grouped = indices.reshape(count // block, block)

    def one_block(wanted):
        selector = (wanted[:, None] == row_ids[None, :]).astype(jnp.float32)
        return jnp.dot(
            selector, table, precision=lax.Precision.HIGHEST, preferred_element_type=jnp.float32
        )

    return lax.map(one_block, grouped).reshape(count, table.shape[1])


def body(tables, cold_rows, cold_bags, hot_rows, hot_ids):
    axis_x = lax.axis_size("gx")
    axis_y = lax.axis_size("gy")
    peer_count = axis_x * axis_y
    table_count, rows_dev, emb_width = tables.shape
    slot_cap = cold_rows.shape[3]
    batch_rows = hot_ids.shape[0]
    hot_count = hot_rows.shape[1]
    my_index = lax.axis_index(("gx", "gy"))
    hot_owner = hot_rows // rows_dev
    local_rows = jnp.where(hot_owner == my_index, hot_rows - my_index * rows_dev, -1)
    picked = jax.vmap(pick_rows)(tables, local_rows)
    hot_table = lax.psum(picked, ("gx", "gy"))
    matches = jnp.sum(
        (
            hot_ids[:, :, :, None] == jnp.arange(hot_count, dtype=jnp.int32)[None, None, None, :]
        ).astype(jnp.float32),
        axis=2,
    )
    hot_part = jnp.einsum("bth,thd->btd", matches, hot_table, precision=lax.Precision.HIGHEST)
    my_rows = cold_rows[0]
    my_bags = cold_bags[0]
    got_rows, got_bags = (
        lax.all_to_all(my_rows, ("gx", "gy"), split_axis=1, concat_axis=1, tiled=True),
        lax.all_to_all(my_bags, ("gx", "gy"), split_axis=1, concat_axis=1, tiled=True),
    )
    wanted_rows = jnp.where(got_bags >= 0, got_rows, -1)
    looked = jax.vmap(pick_rows)(tables, wanted_rows.reshape(table_count, -1))
    looked = looked.reshape(table_count, peer_count, slot_cap, emb_width)
    samples = jnp.arange(batch_rows, dtype=jnp.int32)
    returned = lax.all_to_all(looked, ("gx", "gy"), split_axis=1, concat_axis=1, tiled=True)
    onehot = (my_bags[:, None, :, :] == samples[None, :, None, None]).astype(jnp.float32)
    cold_part = jnp.einsum("tbpc,tpcd->btd", onehot, returned, precision=lax.Precision.HIGHEST)
    return cold_part + hot_part


def solution(mesh):
    return jax.shard_map(
        body,
        mesh=mesh,
        in_specs=(
            P(None, ("gx", "gy"), None),
            P(("gx", "gy"), None, None, None),
            P(("gx", "gy"), None, None, None),
            P(),
            P(("gx", "gy"), None, None),
        ),
        out_specs=P(("gx", "gy"), None, None),
        check_vma=False,
    )
```

profile of v0, /device:TPU:0, one launch (start us, length us, event | category | flops | bytes accessed | tf_op | source)
XLA Modules:
  0.0 203.2 jit_solution(9199264976657592994)
XLA Ops:
  6.5 1.4 copy.23
  7.9 7.3 %all-to-all-start.1 = ((s32[2,32,16]{2,0,1:T(2,128)}), s32[2,32,16]{2,0,1:T(2,128)S(1)}, u32[]{:S(2)}, u32[]{:S(2)}) async-start(s32[2,32,16]{2,0,1:T(2,128)} %bitcast.1), calls=%async_computation.1 | async-start | bytes 65536 | tf_op jit(solution)/shard_map/all_to_all | solution.py:46
  15.3 1.4 copy.22
  16.7 5.9 %all-to-all-done.1 = s32[2,32,16]{2,0,1:T(2,128)S(1)} async-done(((s32[2,32,16]{2,0,1:T(2,128)}), s32[2,32,16]{2,0,1:T(2,128)S(1)}, u32[]{:S(2)}, u32[]{:S(2)}) %all-to-all-start.1) | async-done | bytes 4128 | tf_op jit(solution)/shard_map/all_to_all | solution.py:46
  22.5 2.6 %all-to-all-start = ((s32[2,32,16]{2,0,1:T(2,128)}), s32[2,32,16]{2,0,1:T(2,128)S(1)}, u32[]{:S(2)}, u32[]{:S(2)}) async-start(s32[2,32,16]{2,0,1:T(2,128)} %bitcast), calls=%async_computation | async-start | bytes 65536 | tf_op jit(solution)/shard_map/all_to_all | solution.py:47
  25.1 7.2 %all-to-all-done = s32[2,32,16]{2,0,1:T(2,128)S(1)} async-done(((s32[2,32,16]{2,0,1:T(2,128)}), s32[2,32,16]{2,0,1:T(2,128)S(1)}, u32[]{:S(2)}, u32[]{:S(2)}) %all-to-all-start) | async-done | bytes 4128 | tf_op jit(solution)/shard_map/all_to_all | solution.py:47
  32.4 0.1 eq.74
  32.5 0.0 copy-start.1
  32.5 18.0 %fusion = f32[2,512,128]{2,1,0:T(8,128)S(1)} fusion(f32[2,8192,128]{2,1,0:T(8,128)} %param.5, s32[2,512]{1,0:T(2,128)S(1)} %eq.74), kind=kOutput, calls=%fused_computation.1 | convolution fusion | flops 12893290496 | bytes 8916992 | tf_op jit(solution)/shard_map/vmap()/while/body/eval_jaxpr/dot_general | solution.py:16
  50.5 0.0 copy-start
  50.5 0.9 copy.25
  51.4 2.6 %all-to-all-start.2 = ((f32[2,32,16,128]{3,2,0,1:T(8,128)}), f32[2,32,16,128]{3,2,0,1:T(8,128)S(1)}, u32[]{:S(2)}, u32[]{:S(2)}) async-start(f32[2,32,16,128]{3,2,0,1:T(8,128)} %copy.25), calls=%async_computation.2 | async-start | bytes 1048576 | tf_op jit(solution)/shard_map/all_to_all | solution.py:53
  54.0 0.2 all-reduce.2.cloned.1.call-start
  54.2 0.0 copy-done.1
  54.3 11.7 %fusion.2 = f32[2,256,128]{2,1,0:T(8,128)} fusion(f32[2,8192,128]{2,1,0:T(8,128)} %param.5, s32[2,256]{1,0:T(2,128)S(1)} %compare_select_fusion.1), kind=kOutput, calls=%fused_computation.4 | convolution fusion | flops 6446645248 | bytes 8652800 | tf_op jit(solution)/shard_map/vmap()/while/body/eval_jaxpr/dot_general | solution.py:16
  66.0 0.0 all-reduce.2.cloned.1.call-update
  66.0 0.0 copy-done
  66.0 0.1 copy.26
  66.2 0.8 convert_reduce_fusion
  67.0 2.6 %all-to-all-done.2 = f32[2,32,16,128]{3,2,0,1:T(8,128)S(1)} async-done(((f32[2,32,16,128]{3,2,0,1:T(8,128)}), f32[2,32,16,128]{3,2,0,1:T(8,128)S(1)}, u32[]{:S(2)}, u32[]{:S(2)}) %all-to-all-start.2) | async-done | bytes 524320 | tf_op jit(solution)/shard_map/all_to_all | solution.py:53
  69.6 1.5 convolution_bitcast_fusion
  71.1 122.8 %all-reduce.2.cloned.1.call-done = f32[2,256,128]{2,1,0:T(8,128)} async-done(((f32[2,256,128]{2,1,0:T(8,128)}), f32[2,256,128]{2,1,0:T(8,128)}) %all-reduce.2.cloned.1.call-update) | async-done | bytes 262160 | tf_op jit(solution)/shard_map/psum | solution.py:35
  194.0 1.6 fusion.4
  195.6 0.8 copy.29
  (3 shorter events, 0.0 us)
Async XLA Ops:
  7.9 14.6 %all-to-all-start.1 = ((s32[2,32,16]{2,0,1:T(2,128)}), s32[2,32,16]{2,0,1:T(2,128)S(1)}, u32[]{:S(2)}, u32[]{:S(2)}) async-start(s32[2,32,16]{2,0,1:T(2,128)} %bitcast.1), calls=%async_computation.1 | async-start | bytes 65536 | tf_op jit(solution)/shard_map/all_to_all | solution.py:46
  22.5 9.8 %all-to-all-start = ((s32[2,32,16]{2,0,1:T(2,128)}), s32[2,32,16]{2,0,1:T(2,128)S(1)}, u32[]{:S(2)}, u32[]{:S(2)}) async-start(s32[2,32,16]{2,0,1:T(2,128)} %bitcast), calls=%async_computation | async-start | bytes 65536 | tf_op jit(solution)/shard_map/all_to_all | solution.py:47
  32.5 21.8 %copy-start.1 = (s32[2,256]{1,0:T(2,128)S(1)}, s32[2,256]{1,0:T(2,128)}, u32[]{:S(2)}) copy-start(s32[2,256]{1,0:T(2,128)} %param.8) | copy-start | bytes 6148
  50.5 15.5 %copy-start = (s32[128,2,8]{0,2,1:T(8,128)S(1)}, s32[128,2,8]{0,2,1:T(8,128)}, u32[]{:S(2)}) copy-start(s32[128,2,8]{0,2,1:T(8,128)} %param.9) | copy-start | bytes 24580
  51.4 18.2 %all-to-all-start.2 = ((f32[2,32,16,128]{3,2,0,1:T(8,128)}), f32[2,32,16,128]{3,2,0,1:T(8,128)S(1)}, u32[]{:S(2)}, u32[]{:S(2)}) async-start(f32[2,32,16,128]{3,2,0,1:T(8,128)} %copy.25), calls=%async_computation.2 | async-start | bytes 1048576 | tf_op jit(solution)/shard_map/all_to_all | solution.py:53
  54.0 140.0 %all-reduce.2.cloned.1.call-start = ((), (), s32[]{:S(2)}) async-start(), calls=%async_computation.3 | async-start | bytes 524288 | tf_op jit(solution)/shard_map/psum | solution.py:35
Sparse Core Ops, SparseCore 0:
  66.1 127.7 all-reduce.1
where the time goes:
time: 204 us; the launch traced here: 203 us
  waiting for transfers between devices  139 us (68%)
  matrix products  32.8 us (16%)
  between operations  13.5 us (7%)
  starting transfers between devices  12.7 us (6%)
  local copies, waits for them, and re-layouts  4.66 us (2%)
    psum x1, waiting for transfers between devices, body(): hot_table = lax.psum(picked, ('gx', 'gy'))  123 us
    dot_general x2, matrix products, one_block(): jnp.dot(selector, table, precision=lax.Precision.HIGHEST, preferred_eleme...  29.7 us
    all_to_all x1, starting transfers between devices, body(): lax.all_to_all(my_rows, ('gx', 'gy'), split_axis=1, concat_axis=1, tiled=...  7.33 us
    all_to_all x1, waiting for transfers between devices, body(): lax.all_to_all(my_bags, ('gx', 'gy'), split_axis=1, concat_axis=1, tiled=...  7.25 us
    all_to_all x1, waiting for transfers between devices, body(): lax.all_to_all(my_rows, ('gx', 'gy'), split_axis=1, concat_axis=1, tiled=...  5.86 us
  transfers between devices with their start and end apart: 4, of which 4 were waited for; matrix products, arithmetic and copies ran while one was open for 8% of the time, Pallas kernels for 0%

commit v1 on v0

--- a/solution.py
+++ b/solution.py
@@ -32,7 +32,7 @@
     hot_owner = hot_rows // rows_dev
     local_rows = jnp.where(hot_owner == my_index, hot_rows - my_index * rows_dev, -1)
     picked = jax.vmap(pick_rows)(tables, local_rows)
-    hot_table = lax.psum(picked, ("gx", "gy"))
+    hot_table = jnp.sum(lax.all_gather(picked, ("gx", "gy")), axis=0)
     matches = jnp.sum(
         (
             hot_ids[:, :, :, None] == jnp.arange(hot_count, dtype=jnp.int32)[None, None, None, :]

time: 204 us -> 117 us (0.57)
  waiting for transfers between devices: 139 us -> 44.3 us
  blocking collectives: 0 us -> 9 us
  other arithmetic: 0.86 us -> 5.35 us
  starting transfers between devices: 12.7 us -> 9.93 us
    psum x1 -> x0, waiting for transfers between devices: 123 us -> none  [body(): hot_table = lax.psum(picked, ('gx', 'gy'))]
    all_to_all x1, waiting for transfers between devices: 2.63 us -> 24.6 us  [body(): lax.all_to_all(looked, ('gx', 'gy'), split_axis=1, concat_axis=1, tiled=T...]
    all_gather x0 -> x1, waiting for transfers between devices: none -> 12.6 us  [body(): hot_table = jnp.sum(lax.all_gather(picked, ('gx', 'gy')), axis=0)]
    all_to_all x0 -> x1, blocking collectives: none -> 9 us  [body(): lax.all_to_all(my_rows, ('gx', 'gy'), split_axis=1, concat_axis=1, tiled=...]
    all_to_all x1 -> x0, starting transfers between devices: 7.33 us -> none  [body(): lax.all_to_all(my_rows, ('gx', 'gy'), split_axis=1, concat_axis=1, tiled=...]
    all_to_all x1 -> x0, waiting for transfers between devices: 5.86 us -> none  [body(): lax.all_to_all(my_rows, ('gx', 'gy'), split_axis=1, concat_axis=1, tiled=...]
    all_to_all x1, starting transfers between devices: 2.55 us -> 7.33 us  [body(): lax.all_to_all(my_bags, ('gx', 'gy'), split_axis=1, concat_axis=1, tiled=...]
    reduce_sum x0 -> x1, other arithmetic: none -> 3.79 us  [body(): hot_table = jnp.sum(lax.all_gather(picked, ('gx', 'gy')), axis=0)]
  transfers between devices with their start and end apart: 4 -> 3, of which waited for: 4 -> 3; matrix products, arithmetic and copies ran while one was open for 8% -> 19% of each run, Pallas kernels for 0% -> 0%
where the time goes in v1:
time: 117 us
  waiting for transfers between devices  44.3 us (38%)
  matrix products  31.9 us (27%)
  between operations  13.5 us (12%)
  starting transfers between devices  9.93 us (8%)
  blocking collectives  9 us (8%)
  other arithmetic  5.35 us (5%)
  local copies, waits for them, and re-layouts  2.69 us (2%)
    dot_general x2, matrix products, one_block(): jnp.dot(selector, table, precision=lax.Precision.HIGHEST, preferred_eleme...  29.7 us
    all_to_all x1, waiting for transfers between devices, body(): lax.all_to_all(looked, ('gx', 'gy'), split_axis=1, concat_axis=1, tiled=T...  24.6 us
    all_gather x1, waiting for transfers between devices, body(): hot_table = jnp.sum(lax.all_gather(picked, ('gx', 'gy')), axis=0)  12.6 us
    all_to_all x1, blocking collectives, body(): lax.all_to_all(my_rows, ('gx', 'gy'), split_axis=1, concat_axis=1, tiled=...  9 us
    all_to_all x1, starting transfers between devices, body(): lax.all_to_all(my_bags, ('gx', 'gy'), split_axis=1, concat_axis=1, tiled=...  7.33 us
    all_to_all x1, waiting for transfers between devices, body(): lax.all_to_all(my_bags, ('gx', 'gy'), split_axis=1, concat_axis=1, tiled=...  7.17 us
    reduce_sum x1, other arithmetic, body(): hot_table = jnp.sum(lax.all_gather(picked, ('gx', 'gy')), axis=0)  3.79 us
    all_to_all x1, starting transfers between devices, body(): lax.all_to_all(looked, ('gx', 'gy'), split_axis=1, concat_axis=1, tiled=T...  2.6 us
  transfers between devices with their start and end apart: 3, of which 3 were waited for; matrix products, arithmetic and copies ran while one was open for 19% of the time, Pallas kernels for 0%

profile of v1, /device:TPU:0, one launch (start us, length us, event | category | flops | bytes accessed | tf_op | source)
XLA Modules:
  0.0 116.7 jit_solution(8866116060832862002)
XLA Ops:
  6.5 0.0 copy-start
  6.5 0.0 copy-start.1
  6.5 0.0 all-gather.3.cloned.1.call-start
  6.5 0.7 compare_select_fusion.1
  7.3 11.7 %fusion.2 = f32[2,256,128]{2,1,0:T(8,128)} fusion(f32[2,8192,128]{2,1,0:T(8,128)} %param.5, s32[2,256]{1,0:T(2,128)S(1)} %compare_select_fusion.1), kind=kOutput, calls=%fused_computation.4 | convolution fusion | flops 6446645248 | bytes 8652800 | tf_op jit(solution)/shard_map/vmap()/while/body/eval_jaxpr/dot_general | solution.py:16
  19.0 0.0 all-gather.3.cloned.1.call-update
  19.0 0.0 copy-done
  19.0 0.7 copy.22
  19.7 7.3 %all-to-all-start = ((s32[2,32,16]{2,0,1:T(2,128)}), s32[2,32,16]{2,0,1:T(2,128)S(1)}, u32[]{:S(2)}, u32[]{:S(2)}) async-start(s32[2,32,16]{2,0,1:T(2,128)} %bitcast), calls=%async_computation | async-start | bytes 65536 | tf_op jit(solution)/shard_map/all_to_all | solution.py:47
  27.0 0.0 copy-done.1
  27.0 0.1 copy.23
  27.1 7.2 %all-to-all-done = s32[2,32,16]{2,0,1:T(2,128)S(1)} async-done(((s32[2,32,16]{2,0,1:T(2,128)}), s32[2,32,16]{2,0,1:T(2,128)S(1)}, u32[]{:S(2)}, u32[]{:S(2)}) %all-to-all-start) | async-done | bytes 4128 | tf_op jit(solution)/shard_map/all_to_all | solution.py:47
  34.3 9.0 %all_to_all.15 = s32[2,32,16]{2,0,1:T(2,128)S(1)} all-to-all(s32[2,32,16]{2,0,1:T(2,128)S(1)} %bitcast.14), channel_id=1, replica_groups=mesh['gx'=4,'gy'=8] {'gx','gy'}, dimensions={1} | all-to-all | bytes 8192 | tf_op jit(solution)/shard_map/all_to_all | solution.py:46
  43.3 0.1 eq.74
  43.4 0.0 copy-start.2
  43.4 18.0 %fusion = f32[2,512,128]{2,1,0:T(8,128)S(1)} fusion(f32[2,8192,128]{2,1,0:T(8,128)} %param.5, s32[2,512]{1,0:T(2,128)S(1)} %eq.74), kind=kOutput, calls=%fused_computation.1 | convolution fusion | flops 12893290496 | bytes 8916992 | tf_op jit(solution)/shard_map/vmap()/while/body/eval_jaxpr/dot_general | solution.py:16
  61.5 0.9 copy.25
  62.4 2.6 %all-to-all-start.2 = ((f32[2,32,16,128]{3,2,0,1:T(8,128)}), f32[2,32,16,128]{3,2,0,1:T(8,128)S(1)}, u32[]{:S(2)}, u32[]{:S(2)}) async-start(f32[2,32,16,128]{3,2,0,1:T(8,128)} %copy.25), calls=%async_computation.2 | async-start | bytes 1048576 | tf_op jit(solution)/shard_map/all_to_all | solution.py:53
  65.0 0.0 copy-done.2
  65.0 0.1 copy.26
  65.1 0.8 convert_reduce_fusion
  66.0 24.6 %all-to-all-done.2 = f32[2,32,16,128]{3,2,0,1:T(8,128)S(1)} async-done(((f32[2,32,16,128]{3,2,0,1:T(8,128)}), f32[2,32,16,128]{3,2,0,1:T(8,128)S(1)}, u32[]{:S(2)}, u32[]{:S(2)}) %all-to-all-start.2) | async-done | bytes 524320 | tf_op jit(solution)/shard_map/all_to_all | solution.py:53
  90.6 1.5 %convolution_bitcast_fusion = f32[2,128,128]{2,1,0:T(8,128)S(1)} fusion(f32[2,32,16,128]{3,2,0,1:T(8,128)S(1)} %all-to-all-done.2, s32[2,32,16]{2,0,1:T(2,128)} %bitcast), kind=kOutput, calls=%fused_computation.10 | convolution fusion | flops 201457664 | bytes 659456 | tf_op jit(solution)/shard_map/tbpc,tpcd->btd/dot_general | solution.py:55
  92.1 12.6 %all-gather.3.cloned.1.call-done = f32[64,256,128]{2,1,0:T(8,128)} async-done(((f32[2,256,128]{2,1,0:T(8,128)}), f32[64,256,128]{2,1,0:T(8,128)}) %all-gather.3.cloned.1.call-update) | async-done | bytes 8388624 | tf_op jit(solution)/shard_map/all_gather | solution.py:35
  104.6 3.8 %reduce_sum.18 = f32[2,256,128]{2,1,0:T(8,128)S(1)} reduce(f32[32,2,256,128]{3,2,1,0:T(8,128)} %bitcast.12, f32[]{:T(128)} %constant.49.clone.1), dimensions={0}, to_apply=%region_0.1 | reduce | flops 2031616 | bytes 8650756 | tf_op jit(solution)/shard_map/reduce_sum | solution.py:35
  108.4 0.6 fusion.4
  109.1 0.8 copy.29
  (2 shorter events, 0.0 us)
Async XLA Ops:
  6.5 12.5 %copy-start = (s32[1,2,32,16]{2,3,1,0:T(8,128)S(1)}, s32[1,2,32,16]{2,3,1,0:T(8,128)}, u32[]{:S(2)}) copy-start(s32[1,2,32,16]{2,3,1,0:T(8,128)} %param.7) | copy-start | bytes 12292
  6.5 20.5 %copy-start.1 = (s32[1,2,32,16]{2,3,1,0:T(8,128)S(1)}, s32[1,2,32,16]{2,3,1,0:T(8,128)}, u32[]{:S(2)}) copy-start(s32[1,2,32,16]{2,3,1,0:T(8,128)} %param.6) | copy-start | bytes 12292
  6.5 98.1 %all-gather.3.cloned.1.call-start = ((), (), s32[]{:S(2)}) async-start(), calls=%async_computation.3 | async-start | bytes 8650752 | tf_op jit(solution)/shard_map/all_gather | solution.py:35
  19.7 14.6 %all-to-all-start = ((s32[2,32,16]{2,0,1:T(2,128)}), s32[2,32,16]{2,0,1:T(2,128)S(1)}, u32[]{:S(2)}, u32[]{:S(2)}) async-start(s32[2,32,16]{2,0,1:T(2,128)} %bitcast), calls=%async_computation | async-start | bytes 65536 | tf_op jit(solution)/shard_map/all_to_all | solution.py:47
  43.4 21.6 %copy-start.2 = (s32[128,2,8]{0,2,1:T(8,128)S(1)}, s32[128,2,8]{0,2,1:T(8,128)}, u32[]{:S(2)}) copy-start(s32[128,2,8]{0,2,1:T(8,128)} %param.9) | copy-start | bytes 24580
  62.4 28.2 %all-to-all-start.2 = ((f32[2,32,16,128]{3,2,0,1:T(8,128)}), f32[2,32,16,128]{3,2,0,1:T(8,128)S(1)}, u32[]{:S(2)}, u32[]{:S(2)}) async-start(f32[2,32,16,128]{3,2,0,1:T(8,128)} %copy.25), calls=%async_computation.2 | async-start | bytes 1048576 | tf_op jit(solution)/shard_map/all_to_all | solution.py:53
Sparse Core Ops, SparseCore 0:
  19.1 85.4 all-gather.2
